TPU v7x, 32 devices: a whole 2x2x4 slice. The times are simulated.
32 devices in a mesh: tok: 8 (over y, x, core), exp: 4 (over z).
Axes of the slice: x: 2, y: 2, z: 4, core: 2. Of those that a mesh axis runs over, the one named last changes fastest.
Arguments:
- expert_rows: bfloat16 [4, 2048, 4096], P('exp', 'tok'), may hold values from -480 to 480
- router_input: bfloat16 [2048, 4096], P(('tok', 'exp')), may hold values from -6 to 6
- router_weight: float32 [4096, 4], replicated, may hold values from -0.09375 to 0.09375
- assign: int32 [2048, 2], P(('tok', 'exp')), may hold values from 0 to 3, all different within a row
- targets: int32 [2048], P(('tok', 'exp')), may hold values from 0 to 15999
- head: bfloat16 [4096, 16000], P('tok', 'exp'), may hold values from -0.35 to 0.35
Outputs:
- token_loss: float32 [2048], P(('tok', 'exp'))
- router_grad: float32 [4096, 4], replicated
- mean_loss: float32 [], replicated
All inputs are finite; a program needn't handle non-finite values.
Results may differ from a plain program's by a relative error of at most 0.007.
Values may be sent and summed in bfloat16 or wider, within the bound.
A program may use at most 128 MiB of HBM per device.

v0:
```python
import math
import jax
import jax.numpy as jnp
from jax import lax
from jax.sharding import PartitionSpec as P


def shards(expert_rows, router_input, router_weight, assign, targets, head):
    experts = router_weight.shape[1]
    own_rows = router_input.shape[0]
    tokens_all = own_rows * lax.axis_size("tok") * lax.axis_size("exp")
    loss_scale = 1.0 / math.sqrt(tokens_all)
    inputs = router_input.astype(jnp.float32)
    gate_logits = jnp.dot(inputs, router_weight, precision=lax.Precision.HIGHEST)
    labels = jnp.arange(experts, dtype=jnp.int32)
    first_hot = (assign[:, 0:1] == labels[None, :]).astype(jnp.float32)
    second_hot = (assign[:, 1:2] == labels[None, :]).astype(jnp.float32)
    differ = first_hot - second_hot
    mix_share = jax.nn.sigmoid(jnp.sum(gate_logits * differ, axis=1))
    mixing = mix_share[:, None] * first_hot + (1.0 - mix_share)[:, None] * second_hot
    local_rows = lax.all_to_all(expert_rows, "exp", split_axis=1, concat_axis=0, tiled=True)
    local_wide = local_rows.astype(jnp.float32)
    mixed_own = jnp.sum(mixing.T[:, :, None] * local_wide, axis=0).astype(jnp.bfloat16)
    mixed_rows, group_targets = (
        lax.all_gather(mixed_own, "exp", axis=0, tiled=True),
        lax.all_gather(targets, "exp", axis=0, tiled=True),
    )
    shard_width = head.shape[1]
    full_head = lax.all_gather(head, "tok", axis=0, tiled=True)
    logits = jnp.dot(mixed_rows, full_head, preferred_element_type=jnp.float32)
    first_col = lax.axis_index("exp") * shard_width
    columns = first_col + jnp.arange(shard_width, dtype=jnp.int32)
    target_hit = group_targets[:, None] == columns[None, :]
    picked = jnp.sum(jnp.where(target_hit, logits, 0.0), axis=1)
    local_top = jnp.max(logits, axis=1)
    row_top = lax.pmax(local_top, "exp")
    exp_total, target_logit = lax.psum(
        (jnp.sum(jnp.exp(logits - row_top[:, None]), axis=1), picked), "exp"
    )
    log_total = row_top + jnp.log(exp_total)
    group_loss = log_total - target_logit
    own_loss = lax.dynamic_slice_in_dim(group_loss, lax.axis_index("exp") * own_rows, own_rows, 0)
    loss_sum = lax.psum(jnp.sum(own_loss), ("tok", "exp"))
    slope = (
        loss_scale * (jnp.exp(logits - log_total[:, None]) - target_hit.astype(jnp.float32))
    ).astype(jnp.bfloat16)
    hidden_slope = lax.psum_scatter(
        lax.dot_general(
            slope, full_head, (((1,), (1,)), ((), ())), preferred_element_type=jnp.float32
        ).astype(jnp.bfloat16),
        "exp",
        scatter_dimension=0,
        tiled=True,
    ).astype(jnp.float32)
    weight_slope = jnp.sum(hidden_slope[None, :, :] * local_wide, axis=2).T
    spread = jnp.sum(weight_slope * differ, axis=1) * mix_share * (1.0 - mix_share)
    gate_slope = spread[:, None] * differ
    router_part = jnp.dot(inputs.T, gate_slope, precision=lax.Precision.HIGHEST)
    router_sum = lax.psum(router_part, ("tok", "exp"))
    mean_loss = loss_sum / tokens_all
    return (own_loss, router_sum, mean_loss)


def solution(mesh):
    in_specs = (
        P("exp", "tok", None),
        P(("tok", "exp"), None),
        P(),
        P(("tok", "exp"), None),
        P(("tok", "exp")),
        P("tok", "exp"),
    )
    out_specs = (P(("tok", "exp")), P(), P())
    return jax.shard_map(shards, mesh=mesh, in_specs=in_specs, out_specs=out_specs, check_vma=False)
```

profile of v0, /device:TPU:1, one launch (start us, length us, event | category | flops | bytes accessed | tf_op | source)
XLA Modules:
  0.0 542.0 jit_solution(5459968139769704115)
XLA Ops:
  7.2 0.0 copy-start
  7.2 8.4 %copy.16 = bf16[1,256,4096]{2,0,1:T(2,128)(2,1)} copy(bf16[1,256,4096]{2,1,0:T(8,128)(2,1)} %param.6) | data formatting | bytes 4194304 | tf_op args[0]
  15.6 0.5 broadcast.107
  16.1 13.5 %reduce.1 = bf16[256,4096]{1,0:T(8,128)(2,1)S(1)} reduce(bf16[256,1,4096]{2,1,0:T(2,128)(2,1)} %bitcast.29, bf16[]{:T(256)} %broadcast.107), dimensions={1}, to_apply=%bitcast.25.reduce_sub_computation | reduce | bytes 4194306
  29.6 0.0 copy-start.3
  29.6 0.0 copy-start.2
  29.6 2.8 reshape.110
  32.4 5.4 all-to-all-start
  37.8 0.0 all-gather.3.cloned.1.call-start
  37.8 0.0 copy-done.3
  37.8 0.0 copy-done
  37.8 0.0 copy-done.2
  37.9 0.5 fusion.10
  38.4 47.2 %all-to-all-done = bf16[4,2,131072]{2,1,0:T(2,128)(2,1)S(1)} async-done(((bf16[4,2,131072]{2,1,0:T(2,128)(2,1)}), bf16[4,2,131072]{2,1,0:T(2,128)(2,1)S(1)}, u32[]{:S(2)}, u32[]{:S(2)}) %all-to-all-start) | async-done | bytes 2097184 | tf_op jit(solution)/shard_map/all_to_all | solution.py:21
  85.6 3.3 reshape.111
  88.9 6.0 %copy_convert_fusion = f32[1,256,4096]{2,1,0:T(8,128)S(1)} fusion(bf16[1,256,4096]{2,0,1:T(2,128)(2,1)} %bitcast.27), kind=kLoop, calls=%fused_computation.12 | loop fusion | flops 1048576 | bytes 6291456 | tf_op jit(solution)/shard_map/convert_element_type | solution.py:22
  94.9 0.0 copy-start.5
  94.9 0.0 copy-start.4
  94.9 1.4 multiply_reduce_fusion
  96.3 0.0 all-gather.3.cloned.1.call-update
  96.3 0.0 all-gather.5.cloned.1.call-start
  96.3 0.7 all-gather.5.cloned.1.call-update
  97.1 0.2 reduce-scatter.2.cloned.1.call-start
  97.3 0.0 copy-done.5
  97.3 0.6 dynamic-slice
  98.5 0.0 copy-done.4
  98.6 0.2 dynamic-update-slice
  98.8 4.0 all-reduce
  102.8 39.0 %all-gather.3.cloned.1.call-done = bf16[256,4096]{1,0:T(8,128)(2,1)} async-done(((bf16[64,4096]{1,0:T(8,128)(2,1)}), bf16[256,4096]{1,0:T(8,128)(2,1)}) %all-gather.3.cloned.1.call-update) | async-done | bytes 2097168 | tf_op jit(solution)/shard_map/all_gather | solution.py:25
  141.8 165.1 %all-gather.5.cloned.1.call-done = bf16[4096,4000]{0,1:T(8,128)(2,1)} async-done(((bf16[512,4000]{0,1:T(8,128)(2,1)}), bf16[4096,4000]{0,1:T(8,128)(2,1)}) %all-gather.5.cloned.1.call-update) | async-done | bytes 32768016 | tf_op jit(solution)/shard_map/all_gather | solution.py:29
  306.9 16.2 %fusion.19 = (f32[256]{0:T(256)S(1)}, f32[256,4000]{0,1:T(8,128)}) fusion(bf16[256,4096]{1,0:T(8,128)(2,1)} %all-gather.3.cloned.1.call-done, bf16[4096,4000]{0,1:T(8,128)(2,1)} %all-gather.5.cloned.1.call-done), kind=kOutput, calls=%fused_computation.41 | convolution fusion | flops 8389632000 | bytes 38962176 | tf_op jit(solution)/shard_map/dot_general | solution.py:30
  323.2 9.7 %pmax.7 = f32[256]{0:T(256)S(1)} all-reduce(f32[256]{0:T(256)S(1)} %get-tuple-element.15), channel_id=1, replica_groups=mesh['tok'=8,'exp'=4] {'exp'}, use_global_device_ids=true, to_apply=%region_3.4 | all-reduce | flops 256 | bytes 2048 | tf_op jit(solution)/shard_map/pmax | solution.py:36
  332.8 3.9 fusion.1
  336.7 6.6 %all-reduce.1 = (f32[256]{0:T(256)S(1)}, f32[256]{0:T(256)S(1)}) all-reduce(f32[256]{0:T(256)S(1)} %get-tuple-element.4, f32[256]{0:T(256)S(1)} %get-tuple-element.3), channel_id=1, replica_groups=mesh['tok'=8,'exp'=4] {'exp'}, use_global_device_ids=true, to_apply=%region_5.6 | all-reduce | flops 512 | bytes 4096 | tf_op jit(solution)/shard_map/psum | solution.py:37
  343.3 17.2 %convolution_convert_fusion = bf16[256,4096]{1,0:T(8,128)(2,1)} fusion(bf16[4096,4000]{0,1:T(8,128)(2,1)} %all-gather.5.cloned.1.call-done, f32[256,4000]{0,1:T(8,128)} %get-tuple-element.16, f32[256]{0:T(256)S(1)} %get-tuple-element.10, s32[256]{0:T(256)S(1)} %all-reduce, s32[4000]{0:T(1024)S(1)} %iota_add_fusion), kind=kOutput, calls=%fused_computation | convolution fusion | flops 8395800576 | bytes 38979200 | tf_op jit(solution)/shard_map/dot_general | solution.py:48
  360.5 0.0 reduce-scatter.2.cloned.1.call-update
  360.5 0.0 all-reduce.4.cloned.1.call-start
  360.6 45.4 %reduce-scatter.2.cloned.1.call-done = bf16[64,4096]{1,0:T(8,128)(2,1)} async-done(((bf16[256,4096]{1,0:T(8,128)(2,1)}), bf16[64,4096]{1,0:T(8,128)(2,1)}) %reduce-scatter.2.cloned.1.call-update) | async-done | bytes 524304 | tf_op jit(solution)/shard_map/reduce_scatter | solution.py:47
  406.0 0.0 copy-start.1
  406.0 1.7 mul.89
  407.6 0.7 copy-done.1
  408.3 2.4 fusion
  410.7 0.1 reduce_sum.70
  410.8 1.0 convolution_bitcast_fusion
  411.8 0.0 all-reduce.4.cloned.1.call-update
  411.8 1.2 fusion.17
  413.0 39.8 %psum.31 = f32[]{:T(128)} all-reduce(f32[]{:T(128)} %get-tuple-element.7), channel_id=1, replica_groups=mesh['tok'=8,'exp'=4] {'tok','exp'}, use_global_device_ids=true, to_apply=%region_13.14 | all-reduce | flops 1 | bytes 8 | tf_op jit(solution)/shard_map/psum | solution.py:43
  453.4 79.5 %all-reduce.4.cloned.1.call-done = f32[4096,4]{0,1:T(4,128)} async-done(((f32[4096,4]{0,1:T(4,128)}), f32[4096,4]{0,1:T(4,128)}) %all-reduce.4.cloned.1.call-update) | async-done | bytes 65552 | tf_op jit(solution)/shard_map/psum | solution.py:59
  532.9 1.5 copy.19
  (8 shorter events, 0.1 us)
Async XLA Ops:
  7.2 30.7 %copy-start = (bf16[64,4096]{1,0:T(8,128)(2,1)S(1)}, bf16[64,4096]{1,0:T(8,128)(2,1)}, u32[]{:S(2)}) copy-start(bf16[64,4096]{1,0:T(8,128)(2,1)} %param.7) | copy-start | bytes 1572868
  29.6 8.2 %copy-start.3 = (s32[64,2]{0,1:T(2,128)S(1)}, s32[64,2]{0,1:T(2,128)}, u32[]{:S(2)}) copy-start(s32[64,2]{0,1:T(2,128)} %param.9) | copy-start | bytes 1540
  29.6 8.2 %copy-start.2 = (f32[4096,4]{0,1:T(4,128)S(1)}, f32[4096,4]{0,1:T(4,128)}, u32[]{:S(2)}) copy-start(f32[4096,4]{0,1:T(4,128)} %param.8) | copy-start | bytes 196612
  32.4 53.2 %all-to-all-start = ((bf16[4,2,131072]{2,1,0:T(2,128)(2,1)}), bf16[4,2,131072]{2,1,0:T(2,128)(2,1)S(1)}, u32[]{:S(2)}, u32[]{:S(2)}) async-start(bf16[4,2,131072]{2,1,0:T(2,128)(2,1)} %reshape.110), calls=%async_computation | async-start | bytes 4194304 | tf_op jit(solution)/shard_map/all_to_all | solution.py:21
  37.8 104.0 %all-gather.3.cloned.1.call-start = ((), (), s32[]{:S(2)}) async-start(), calls=%async_computation.2 | async-start | bytes 2621440 | tf_op jit(solution)/shard_map/all_gather | solution.py:25
  94.9 2.4 copy-start.5
  94.9 3.6 copy-start.4
  96.3 210.6 %all-gather.5.cloned.1.call-start = ((), (), s32[]{:S(2)}) async-start(), calls=%async_computation.3 | async-start | bytes 36864000 | tf_op jit(solution)/shard_map/all_gather | solution.py:29
  97.1 308.9 %reduce-scatter.2.cloned.1.call-start = ((), (), s32[]{:S(2)}) async-start(), calls=%async_computation.4 | async-start | bytes 2621440 | tf_op jit(solution)/shard_map/reduce_scatter | solution.py:47
  360.5 172.3 %all-reduce.4.cloned.1.call-start = ((), (), s32[]{:S(2)}) async-start(), calls=%async_computation.5 | async-start | bytes 131072 | tf_op jit(solution)/shard_map/psum | solution.py:59
  406.0 2.3 copy-start.1
Sparse Core Ops, SparseCore 0:
  96.4 45.3 all-gather.2
  143.6 163.2 all-gather.4
  360.7 45.2 reduce-scatter.1
  412.0 120.8 all-reduce.3
where the time goes:
time: 543 us; the launch traced here: 542 us
  waiting for transfers between devices  377 us (69%)
  blocking collectives  60.1 us (11%)
  matrix products  34.9 us (6%)
  other arithmetic  28.4 us (5%)
  local copies, waits for them, and re-layouts  19.7 us (4%)
  between operations  16.3 us (3%)
  starting transfers between devices  5.71 us (1%)
    all_gather x1, waiting for transfers between devices, shards(): full_head = lax.all_gather(head, 'tok', axis=0, tiled=True)  165 us
    psum x1, waiting for transfers between devices, shards(): router_sum = lax.psum(router_part, ('tok', 'exp'))  79.5 us
    all_to_all x1, waiting for transfers between devices, shards(): lax.all_to_all(expert_rows, 'exp', split_axis=1, concat_axis=0, tiled=True)  47.2 us
    reduce_scatter x1, waiting for transfers between devices, shards(): lax.psum_scatter(lax.dot_general(slope, full_head, (((1,), (1,)), ((), ()...  45.4 us
    psum x1, blocking collectives, shards(): loss_sum = lax.psum(jnp.sum(own_loss), ('tok', 'exp'))  39.8 us
    all_gather x1, waiting for transfers between devices, shards(): lax.all_gather(mixed_own, 'exp', axis=0, tiled=True)  39 us
    unnamed x20, local copies, waits for them, and re-layouts  18 us
    dot_general x1, matrix products, shards(): lax.dot_general(slope, full_head, (((1,), (1,)), ((), ())), preferred_ele...  17.2 us
  transfers between devices with their start and end apart: 5, of which 5 were waited for; matrix products, arithmetic and copies ran while one was open for 0% of the time, Pallas kernels for 0%

commit v1 on v0

--- a/solution.py
+++ b/solution.py
@@ -26,7 +26,17 @@
         lax.all_gather(targets, "exp", axis=0, tiled=True),
     )
     shard_width = head.shape[1]
-    full_head = lax.all_gather(head, "tok", axis=0, tiled=True)
+    q_n = jax.lax.axis_size("tok")
+    by_rank = [head]
+    for pp in range(q_n - 1):
+        by_rank.append(
+            jax.lax.ppermute(by_rank[-1], "tok", [(kk, (kk + 1) % q_n) for kk in range(q_n)])
+        )
+    full_head = jnp.roll(
+        jnp.concatenate(by_rank[::-1], axis=0),
+        (jax.lax.axis_index("tok") + 1) * head.shape[0],
+        axis=0,
+    )
     logits = jnp.dot(mixed_rows, full_head, preferred_element_type=jnp.float32)
     first_col = lax.axis_index("exp") * shard_width
     columns = first_col + jnp.arange(shard_width, dtype=jnp.int32)

time: 543 us -> 644 us (1.19)
  local copies, waits for them, and re-layouts: 19.7 us -> 82.3 us
  blocking collectives: 60.1 us -> 85.7 us
  starting transfers between devices: 5.71 us -> 22.4 us
    ppermute x0 -> x7, waiting for transfers between devices: none -> 240 us  [shards(): jax.lax.ppermute(by_rank[-1], 'tok', [(kk, (kk + 1) % q_n) for kk in rang...]
    all_gather x1 -> x0, waiting for transfers between devices: 165 us -> none  [shards(): full_head = lax.all_gather(head, 'tok', axis=0, tiled=True)]
    unnamed x20 -> x53, local copies, waits for them, and re-layouts: 18 us -> 78.3 us
    all_to_all x1, waiting for transfers between devices: 47.2 us -> 0.01 us  [shards(): lax.all_to_all(expert_rows, 'exp', split_axis=1, concat_axis=0, tiled=True)]
    all_gather x1, waiting for transfers between devices: 39 us -> 0.01 us  [shards(): lax.all_gather(mixed_own, 'exp', axis=0, tiled=True)]
    unnamed x1, blocking collectives: 4.01 us -> 29.1 us
    ppermute x0 -> x7, starting transfers between devices: none -> 17.5 us  [shards(): jax.lax.ppermute(by_rank[-1], 'tok', [(kk, (kk + 1) % q_n) for kk in rang...]
    reduce_scatter x1, waiting for transfers between devices: 45.4 us -> 52.6 us  [shards(): lax.psum_scatter(lax.dot_general(slope, full_head, (((1,), (1,)), ((), ()...]
  transfers between devices with their start and end apart: 5 -> 11, of which waited for: 5 -> 9; matrix products, arithmetic and copies ran while one was open for 0% -> 14% of each run, Pallas kernels for 0% -> 0%
where the time goes in v1:
time: 644 us; the launch traced here: 643 us
  waiting for transfers between devices  372 us (58%)
  blocking collectives  85.7 us (13%)
  local copies, waits for them, and re-layouts  82.3 us (13%)
  matrix products  36.1 us (6%)
  other arithmetic  28.4 us (4%)
  starting transfers between devices  22.4 us (3%)
  between operations  16.3 us (3%)
    ppermute x7, waiting for transfers between devices, shards(): jax.lax.ppermute(by_rank[-1], 'tok', [(kk, (kk + 1) % q_n) for kk in rang...  240 us
    psum x1, waiting for transfers between devices, shards(): router_sum = lax.psum(router_part, ('tok', 'exp'))  79.7 us
    unnamed x53, local copies, waits for them, and re-layouts  78.3 us
    reduce_scatter x1, waiting for transfers between devices, shards(): lax.psum_scatter(lax.dot_general(slope, full_head, (((1,), (1,)), ((), ()...  52.6 us
    psum x1, blocking collectives, shards(): loss_sum = lax.psum(jnp.sum(own_loss), ('tok', 'exp'))  39.8 us
    unnamed x1, blocking collectives  29.1 us
    ppermute x7, starting transfers between devices, shards(): jax.lax.ppermute(by_rank[-1], 'tok', [(kk, (kk + 1) % q_n) for kk in rang...  17.5 us
    dot_general x1, matrix products, shards(): lax.dot_general(slope, full_head, (((1,), (1,)), ((), ())), preferred_ele...  17.5 us
  transfers between devices with their start and end apart: 11, of which 9 were waited for; matrix products, arithmetic and copies ran while one was open for 14% of the time, Pallas kernels for 0%

profile of v1, /device:TPU:1, one launch (start us, length us, event | category | flops | bytes accessed | tf_op | source)
XLA Modules:
  0.0 643.3 jit_solution(12575223155650715881)
XLA Ops:
  7.2 2.6 collective-permute-start
  9.8 44.7 %collective-permute-done = bf16[512,4000]{0,1:T(8,128)(2,1)S(1)} collective-permute-done((bf16[512,4000]{0,1:T(8,128)(2,1)}, bf16[512,4000]{0,1:T(8,128)(2,1)S(1)}, u32[]{:S(2)}, u32[]{:S(2)}) %collective-permute-start) | collective-permute-done | bytes 4096032 | tf_op jit(solution)/shard_map/ppermute | solution.py:33
  54.5 2.1 copy-done.3
  56.6 2.4 collective-permute-start.1
  59.0 44.4 %collective-permute-done.1 = bf16[512,4000]{0,1:T(8,128)(2,1)S(1)} collective-permute-done((bf16[512,4000]{0,1:T(8,128)(2,1)S(1)}, bf16[512,4000]{0,1:T(8,128)(2,1)S(1)}, u32[]{:S(2)}, u32[]{:S(2)}) %collective-permute-start.1) | collective-permute-done | bytes 4096032 | tf_op jit(solution)/shard_map/ppermute | solution.py:33
  103.4 2.0 copy-done.5
  105.4 2.5 collective-permute-start.2
  107.9 44.4 %collective-permute-done.2 = bf16[512,4000]{0,1:T(8,128)(2,1)S(1)} collective-permute-done((bf16[512,4000]{0,1:T(8,128)(2,1)S(1)}, bf16[512,4000]{0,1:T(8,128)(2,1)S(1)}, u32[]{:S(2)}, u32[]{:S(2)}) %collective-permute-start.2) | collective-permute-done | bytes 4096032 | tf_op jit(solution)/shard_map/ppermute | solution.py:33
  152.3 2.0 copy-done.7
  154.3 2.5 collective-permute-start.3
  156.8 44.4 %collective-permute-done.3 = bf16[512,4000]{0,1:T(8,128)(2,1)S(1)} collective-permute-done((bf16[512,4000]{0,1:T(8,128)(2,1)S(1)}, bf16[512,4000]{0,1:T(8,128)(2,1)S(1)}, u32[]{:S(2)}, u32[]{:S(2)}) %collective-permute-start.3) | collective-permute-done | bytes 4096032 | tf_op jit(solution)/shard_map/ppermute | solution.py:33
  201.2 2.1 copy-done.9
  203.3 2.5 collective-permute-start.4
  205.8 44.4 %collective-permute-done.4 = bf16[512,4000]{0,1:T(8,128)(2,1)} collective-permute-done((bf16[512,4000]{0,1:T(8,128)(2,1)S(1)}, bf16[512,4000]{0,1:T(8,128)(2,1)}, u32[]{:S(2)}, u32[]{:S(2)}) %collective-permute-start.4) | collective-permute-done | bytes 4096032 | tf_op jit(solution)/shard_map/ppermute | solution.py:33
  250.2 2.6 collective-permute-start.5
  252.7 8.3 %copy.16 = bf16[1,256,4096]{2,0,1:T(2,128)(2,1)} copy(bf16[1,256,4096]{2,1,0:T(8,128)(2,1)} %param.6) | data formatting | bytes 4194304 | tf_op args[0]
  261.1 0.5 broadcast.108
  261.6 13.5 %reduce.1 = bf16[256,4096]{1,0:T(8,128)(2,1)S(1)} reduce(bf16[256,1,4096]{2,1,0:T(2,128)(2,1)} %bitcast.27, bf16[]{:T(256)} %broadcast.108), dimensions={1}, to_apply=%bitcast.23.reduce_sub_computation | reduce | bytes 4194306
  275.1 2.8 reshape.110
  277.9 4.6 all-to-all-start
  282.5 14.9 %collective-permute-done.5 = bf16[512,4000]{0,1:T(8,128)(2,1)} collective-permute-done((bf16[512,4000]{0,1:T(8,128)(2,1)}, bf16[512,4000]{0,1:T(8,128)(2,1)}, u32[]{:S(2)}, u32[]{:S(2)}) %collective-permute-start.5) | collective-permute-done | bytes 4096032 | tf_op jit(solution)/shard_map/ppermute | solution.py:33
  297.5 2.5 collective-permute-start.6
  299.9 0.6 dynamic-slice
  301.4 29.1 %all-reduce = s32[256]{0:T(256)S(1)} all-reduce(s32[256]{0:T(256)S(1)} %dynamic-update-slice), channel_id=1, replica_groups=mesh['tok'=8,'exp'=4] {'exp'}, use_global_device_ids=true, to_apply=%add | all-reduce | flops 256 | bytes 2048
  330.6 0.5 fusion.17
  331.2 3.3 reshape.111
  334.5 6.0 copy_convert_fusion
  340.5 1.4 multiply_reduce_fusion
  341.9 0.3 reduce-scatter.2.cloned.1.call-start
  342.2 2.5 collective-permute-done.6
  344.7 4.4 constant_dynamic-update-slice_fusion.15
  349.0 4.6 constant_dynamic-update-slice_fusion.14
  353.6 4.6 constant_dynamic-update-slice_fusion.13
  358.2 2.4 constant_dynamic-update-slice_fusion.12
  360.6 1.3 copy-done.8
  361.9 2.4 constant_dynamic-update-slice_fusion.11
  364.2 1.3 copy-done.6
  365.5 2.4 constant_dynamic-update-slice_fusion.10
  367.9 1.3 copy-done.4
  369.2 2.4 constant_dynamic-update-slice_fusion.9
  371.5 1.3 copy-done.2
  372.8 2.2 constant_dynamic-update-slice_fusion.8
  375.1 4.3 constant_dynamic-update-slice_fusion.7
  379.4 4.3 constant_dynamic-update-slice_fusion.6
  383.7 4.3 constant_dynamic-update-slice_fusion.5
  388.1 2.2 constant_dynamic-update-slice_fusion.4
  390.2 2.2 constant_dynamic-update-slice_fusion.3
  392.4 2.2 constant_dynamic-update-slice_fusion.2
  394.6 2.2 constant_dynamic-update-slice_fusion.1
  396.8 2.2 constant_dynamic-update-slice_fusion
  399.0 17.1 %fusion.28 = (f32[256]{0:T(256)S(1)}, f32[256,4000]{0,1:T(8,128)}) fusion(bf16[256,4096]{1,0:T(8,128)(2,1)} %all-gather.2.cloned.1.call-done, bf16[8192,4000]{0,1:T(8,128)(2,1)} %constant_dynamic-update-slice_fusion, s32[]{:T(128)S(6)} %select_n.21), kind=kOutput, calls=%fused_computation.63 | convolution fusion | flops 8389632000 | bytes 38962180 | tf_op jit(solution)/shard_map/dot_general | solution.py:40
  416.2 9.9 %pmax.7 = f32[256]{0:T(256)S(1)} all-reduce(f32[256]{0:T(256)S(1)} %get-tuple-element.15), channel_id=1, replica_groups=mesh['tok'=8,'exp'=4] {'exp'}, use_global_device_ids=true, to_apply=%region_3.4 | all-reduce | flops 256 | bytes 2048 | tf_op jit(solution)/shard_map/pmax | solution.py:46
  426.1 3.9 fusion.8
  430.0 6.9 %all-reduce.1 = (f32[256]{0:T(256)S(1)}, f32[256]{0:T(256)S(1)}) all-reduce(f32[256]{0:T(256)S(1)} %get-tuple-element.4, f32[256]{0:T(256)S(1)} %get-tuple-element.3), channel_id=1, replica_groups=mesh['tok'=8,'exp'=4] {'exp'}, use_global_device_ids=true, to_apply=%region_5.6 | all-reduce | flops 512 | bytes 4096 | tf_op jit(solution)/shard_map/psum | solution.py:47
  436.9 17.5 %fusion.4 = bf16[256,4096]{1,0:T(8,128)(2,1)} fusion(bf16[8192,4000]{0,1:T(8,128)(2,1)} %constant_dynamic-update-slice_fusion, s32[]{:T(128)S(6)} %select_n.21, f32[256,4000]{0,1:T(8,128)} %get-tuple-element.16, f32[256]{0:T(256)S(1)} %get-tuple-element.10, s32[256]{0:T(256)S(1)} %all-reduce, s32[4000]{0:T(1024)S(1)} %iota_add_fusion), kind=kOutput, calls=%fused_computation.4 | convolution fusion | flops 8395800576 | bytes 38979204 | tf_op jit(solution)/shard_map/dot_general | solution.py:58
  454.4 52.6 %reduce-scatter.2.cloned.1.call-done = bf16[64,4096]{1,0:T(8,128)(2,1)} async-done(((bf16[256,4096]{1,0:T(8,128)(2,1)}), bf16[64,4096]{1,0:T(8,128)(2,1)}) %reduce-scatter.2.cloned.1.call-update) | async-done | bytes 524304 | tf_op jit(solution)/shard_map/reduce_scatter | solution.py:57
  507.1 1.7 mul.93
  508.7 0.7 copy-done.1
  509.4 2.4 fusion.7
  511.9 1.0 convolution_bitcast_fusion
  512.9 1.2 fusion.26
  514.1 39.8 %psum.31 = f32[]{:T(128)} all-reduce(f32[]{:T(128)} %get-tuple-element.7), channel_id=1, replica_groups=mesh['tok'=8,'exp'=4] {'tok','exp'}, use_global_device_ids=true, to_apply=%region_13.14 | all-reduce | flops 1 | bytes 8 | tf_op jit(solution)/shard_map/psum | solution.py:53
  554.5 79.7 %all-reduce.4.cloned.1.call-done = f32[4096,4]{0,1:T(4,128)} async-done(((f32[4096,4]{0,1:T(4,128)}), f32[4096,4]{0,1:T(4,128)}) %all-reduce.4.cloned.1.call-update) | async-done | bytes 65552 | tf_op jit(solution)/shard_map/psum | solution.py:69
  634.2 1.5 copy.34
  (38 shorter events, 0.5 us)
Async XLA Ops:
  7.2 323.4 %copy-start = (bf16[64,4096]{1,0:T(8,128)(2,1)S(1)}, bf16[64,4096]{1,0:T(8,128)(2,1)}, u32[]{:S(2)}) copy-start(bf16[64,4096]{1,0:T(8,128)(2,1)} %param.7) | copy-start | bytes 1572868
  7.2 47.4 %collective-permute-start = (bf16[512,4000]{0,1:T(8,128)(2,1)}, bf16[512,4000]{0,1:T(8,128)(2,1)S(1)}, u32[]{:S(2)}, u32[]{:S(2)}) collective-permute-start(bf16[512,4000]{0,1:T(8,128)(2,1)} %param.11), channel_id=1, source_target_pairs={{0,4},{4,8},{8,12},{12,16},{16,20},{20,24},{24,28},{28,0},{1,5},{5... | collective-permute-start | bytes 12288008 | tf_op jit(solution)/shard_map/ppermute | solution.py:33
  54.5 2.1 copy-start.3
  56.6 46.8 %collective-permute-start.1 = (bf16[512,4000]{0,1:T(8,128)(2,1)S(1)}, bf16[512,4000]{0,1:T(8,128)(2,1)S(1)}, u32[]{:S(2)}, u32[]{:S(2)}) collective-permute-start(bf16[512,4000]{0,1:T(8,128)(2,1)S(1)} %collective-permute-done), channel_id=1, source_target_pairs={{0,4},{4,8},{8,12},{12,16},{16,20},{20,24},{24,28},{28,0},{1,5},{5... | collective-permute-start | bytes 12288008 | tf_op jit(solution)/shard_map/ppermute | solution.py:33
  103.4 2.0 copy-start.5
  105.4 46.9 %collective-permute-start.2 = (bf16[512,4000]{0,1:T(8,128)(2,1)S(1)}, bf16[512,4000]{0,1:T(8,128)(2,1)S(1)}, u32[]{:S(2)}, u32[]{:S(2)}) collective-permute-start(bf16[512,4000]{0,1:T(8,128)(2,1)S(1)} %collective-permute-done.1), channel_id=1, source_target_pairs={{0,4},{4,8},{8,12},{12,16},{16,20},{20,24},{24,28},{28,0},{1,5},{5... | collective-permute-start | bytes 12288008 | tf_op jit(solution)/shard_map/ppermute | solution.py:33
  152.3 2.0 copy-start.7
  154.3 46.9 %collective-permute-start.3 = (bf16[512,4000]{0,1:T(8,128)(2,1)S(1)}, bf16[512,4000]{0,1:T(8,128)(2,1)S(1)}, u32[]{:S(2)}, u32[]{:S(2)}) collective-permute-start(bf16[512,4000]{0,1:T(8,128)(2,1)S(1)} %collective-permute-done.2), channel_id=1, source_target_pairs={{0,4},{4,8},{8,12},{12,16},{16,20},{20,24},{24,28},{28,0},{1,5},{5... | collective-permute-start | bytes 12288008 | tf_op jit(solution)/shard_map/ppermute | solution.py:33
  201.2 2.1 copy-start.9
  203.3 46.9 %collective-permute-start.4 = (bf16[512,4000]{0,1:T(8,128)(2,1)S(1)}, bf16[512,4000]{0,1:T(8,128)(2,1)}, u32[]{:S(2)}, u32[]{:S(2)}) collective-permute-start(bf16[512,4000]{0,1:T(8,128)(2,1)S(1)} %collective-permute-done.3), channel_id=1, source_target_pairs={{0,4},{4,8},{8,12},{12,16},{16,20},{20,24},{24,28},{28,0},{1,5},{5... | collective-permute-start | bytes 12288008 | tf_op jit(solution)/shard_map/ppermute | solution.py:33
  250.2 47.3 %collective-permute-start.5 = (bf16[512,4000]{0,1:T(8,128)(2,1)}, bf16[512,4000]{0,1:T(8,128)(2,1)}, u32[]{:S(2)}, u32[]{:S(2)}) collective-permute-start(bf16[512,4000]{0,1:T(8,128)(2,1)} %collective-permute-done.4), channel_id=1, source_target_pairs={{0,4},{4,8},{8,12},{12,16},{16,20},{20,24},{24,28},{28,0},{1,5},{5... | collective-permute-start | bytes 12288008 | tf_op jit(solution)/shard_map/ppermute | solution.py:33
  275.1 24.8 %copy-start.14 = (u32[32]{0:T(128)S(1)}, u32[32]{0:T(128)}, u32[]{:S(2)}) copy-start(u32[32]{0:T(128)} %constant.58) | copy-start | bytes 388
  275.1 26.1 %copy-start.13 = (s32[64]{0:T(128)S(1)}, s32[64]{0:T(128)}, u32[]{:S(2)}) copy-start(s32[64]{0:T(128)} %param.10) | copy-start | bytes 772
  275.1 55.5 %copy-start.12 = (s32[64,2]{0,1:T(2,128)S(1)}, s32[64,2]{0,1:T(2,128)}, u32[]{:S(2)}) copy-start(s32[64,2]{0,1:T(2,128)} %param.9) | copy-start | bytes 1540
  275.1 55.5 %copy-start.11 = (f32[4096,4]{0,1:T(4,128)S(1)}, f32[4096,4]{0,1:T(4,128)}, u32[]{:S(2)}) copy-start(f32[4096,4]{0,1:T(4,128)} %param.8) | copy-start | bytes 196612
  277.9 53.2 %all-to-all-start = ((bf16[4,2,131072]{2,1,0:T(2,128)(2,1)}), bf16[4,2,131072]{2,1,0:T(2,128)(2,1)S(1)}, u32[]{:S(2)}, u32[]{:S(2)}) async-start(bf16[4,2,131072]{2,1,0:T(2,128)(2,1)} %reshape.110), calls=%async_computation | async-start | bytes 4194304 | tf_op jit(solution)/shard_map/all_to_all | solution.py:21
  282.5 116.5 %all-gather.2.cloned.1.call-start = ((), (), s32[]{:S(2)}) async-start(), calls=%async_computation.2 | async-start | bytes 2621440 | tf_op jit(solution)/shard_map/all_gather | solution.py:25
  297.5 47.2 %collective-permute-start.6 = (bf16[512,4000]{0,1:T(8,128)(2,1)}, bf16[512,4000]{0,1:T(8,128)(2,1)}, u32[]{:S(2)}, u32[]{:S(2)}) collective-permute-start(bf16[512,4000]{0,1:T(8,128)(2,1)} %collective-permute-done.5), channel_id=1, source_target_pairs={{0,4},{4,8},{8,12},{12,16},{16,20},{20,24},{24,28},{28,0},{1,5},{5... | collective-permute-start | bytes 12288008 | tf_op jit(solution)/shard_map/ppermute | solution.py:33
  341.9 165.2 %reduce-scatter.2.cloned.1.call-start = ((), (), s32[]{:S(2)}) async-start(), calls=%async_computation.3 | async-start | bytes 2621440 | tf_op jit(solution)/shard_map/reduce_scatter | solution.py:57
  353.6 4.6 copy-start.10
  358.2 3.7 copy-start.8
  361.9 3.6 copy-start.6
  365.5 3.7 copy-start.4
  369.2 3.7 copy-start.2
  454.4 179.8 %all-reduce.4.cloned.1.call-start = ((), (), s32[]{:S(2)}) async-start(), calls=%async_computation.4 | async-start | bytes 131072 | tf_op jit(solution)/shard_map/psum | solution.py:69
  507.1 2.3 copy-start.1
Sparse Core Ops, SparseCore 0:
  342.0 45.9 all-gather.1
  454.5 52.5 reduce-scatter.1
  513.2 120.9 all-reduce.3
